TPU v7x, 256 devices: a whole 4x4x8 slice. The times are simulated.
256 devices in a mesh: ctx: 8 (over z), vocab: 32 (over y, x, core).
Axes of the slice: x: 4, y: 4, z: 8, core: 2. Of those that a mesh axis runs over, the one named last changes fastest.
Arguments:
- hidden: bfloat16 [16, 128, 4096], P(None, 'ctx', 'vocab'), may hold values from -6 to 6
- head_weight: bfloat16 [4096, 128256], P(None, ('ctx', 'vocab')), may hold values from -0.09375 to 0.09375
- token_ids: int32 [16, 128], P(None, 'ctx'), may hold values from 0 to 128255
- response_mask: int32 [16, 128], P(None, 'ctx'), may hold values 0 or 1
- pair_order: int32 [16], replicated, may hold values from 0 to 15, each once
- frozen_logprob: float32 [16], replicated, may hold values from -40 to 40
Outputs:
- pair_loss: float32 [], replicated
- margins: float32 [8], replicated
- head_grad: bfloat16 [4096, 128256], P(None, ('ctx', 'vocab'))
- spread_grad: bfloat16 [4096, 128256], P(None, ('ctx', 'vocab'))
Inputs may be any that keep to these rules, and one draw needn't show every extreme that they name: `token_ids`: token ids lie in 0 to 128255. `response_mask`: mask entries are 0 or 1. pair_order names every sequence exactly once; entry p is the chosen sequence of pair p and entry 8 + p the rejected one.
All inputs are finite; a program needn't handle non-finite values.
Results may differ from a plain program's by a relative error of at most 0.0015.
Values may be sent and summed in bfloat16 or wider, within the bound.
A program may use at most 128 MiB of HBM per device.

v0:
```python
import jax
import jax.numpy as jnp
from jax import lax
from jax.sharding import Mesh
from jax.sharding import PartitionSpec as P

V = 128256
VOCAB = ("vocab_0", "vocab_1", "vocab_2")
CTX_VOCAB = ("ctx", "vocab_0", "vocab_1", "vocab_2")
strength = 0.1
loss_scale = 256.0


def laid_out(pieces, dim):
    pieces = jnp.moveaxis(pieces, 0, dim)
    lengths = pieces.shape
    return pieces.reshape(*lengths[:dim], lengths[dim] * lengths[dim + 1], *lengths[dim + 2 :])


def gather_packed(arrays, axis, dims):
    flat = jnp.concatenate([a.reshape(-1) for a in arrays])
    lines, at, finished = (lax.all_gather(flat, axis), 0, [])
    for a, dim in zip(arrays, dims):
        pieces = lines[:, at : at + a.size].reshape(-1, *a.shape)
        finished.append(laid_out(pieces, dim))
        at += a.size
    return tuple(finished)


def by_axis(shard, axes):
    for axis in axes:
        shard = lax.pmax(shard, axis)
    return shard


def by_axis_2(shard, axes):
    for axis in axes:
        shard = lax.psum(shard, axis)
    return shard


def contract_rows(block_rows, both_logits):
    return lax.dot_general(
        block_rows, both_logits, (((0,), (0,)), ((), ())), preferred_element_type=jnp.float32
    )


def shards(hidden, head_weight, token_ids, response_mask, pair_order, frozen_logprob):
    seq_rows = lax.all_gather(hidden, "ctx", axis=1, tiled=True)
    ids_all, mask_all = gather_packed((token_ids, response_mask), "ctx", (1, 1))
    token_rows = seq_rows.reshape(seq_rows.shape[0] * seq_rows.shape[1], seq_rows.shape[2])
    shard_width = head_weight.shape[1]
    whole_rows = lax.all_gather(token_rows, VOCAB, axis=1, tiled=True)
    logits = jnp.dot(whole_rows, head_weight, preferred_element_type=jnp.float32)
    offset = lax.axis_index(CTX_VOCAB) * shard_width
    local_ids = ids_all.reshape(-1) - offset
    columns = jnp.arange(shard_width).astype(jnp.int32)
    onehot = (columns[None, :] == local_ids[:, None]).astype(jnp.float32)
    picked_part = jnp.sum(onehot * logits, axis=1)
    peak_part = jnp.max(logits, axis=1)
    row_peak = by_axis(peak_part, CTX_VOCAB)
    exp_sums = jnp.sum(jnp.exp(logits - row_peak[:, None]), axis=1)
    sum_total, picked = (by_axis_2(exp_sums, CTX_VOCAB), by_axis_2(picked_part, CTX_VOCAB))
    log_norm = row_peak + jnp.log(sum_total)
    mask_flat = mask_all.reshape(-1).astype(jnp.float32)
    seq_count = ids_all.shape[0]
    policy = jnp.sum(((picked - log_norm) * mask_flat).reshape(seq_count, ids_all.shape[1]), axis=1)
    log_ratio = policy - frozen_logprob
    pair_count = pair_order.shape[0] // 2
    chosen = pair_order[:pair_count]
    rejected = pair_order[pair_count:]
    margins = strength * (log_ratio[chosen] - log_ratio[rejected])
    pair_loss = jnp.mean(jax.nn.softplus(-margins))
    weight = -loss_scale * strength * jax.nn.sigmoid(-margins) / pair_count
    seq_coef = jnp.zeros((seq_count,), jnp.float32).at[chosen].set(weight).at[rejected].set(-weight)
    token_coef = (seq_coef[:, None] * mask_all.astype(jnp.float32)).reshape(-1)
    probabilities = jnp.exp(logits - log_norm[:, None])
    grad_logits = (token_coef[:, None] * (onehot - probabilities)).astype(jnp.bfloat16)
    spread_logits = (V / 64.0 * token_coef[:, None] * probabilities).astype(jnp.bfloat16)
    both_logits = jnp.concatenate([grad_logits, spread_logits], axis=1)
    both_grads = contract_rows(whole_rows, both_logits)
    head_grad = both_grads[:, :shard_width].astype(jnp.bfloat16)
    spread_grad = both_grads[:, shard_width:].astype(jnp.bfloat16)
    return (pair_loss, margins, head_grad, spread_grad)


def solution(mesh):
    split = Mesh(
        mesh.devices.reshape(mesh.shape["ctx"], 4, 4, 2), ("ctx", "vocab_0", "vocab_1", "vocab_2")
    )
    placed = (P(None, "ctx", VOCAB), P(None, CTX_VOCAB), P(None, "ctx"), P(None, "ctx"), P(), P())
    return jax.shard_map(
        shards,
        mesh=split,
        in_specs=placed,
        out_specs=(P(), P(), P(None, CTX_VOCAB), P(None, CTX_VOCAB)),
        check_vma=False,
    )
```

profile of v0, /device:TPU:1, one launch (start us, length us, event | category | flops | bytes accessed | tf_op | source)
XLA Modules:
  0.0 282.0 jit_solution(17380326910799111413)
XLA Ops:
  7.2 26.5 %all_gather.14 = bf16[16,128,128]{2,1,0:T(8,128)(2,1)} all-gather(bf16[16,16,128]{2,1,0:T(8,128)(2,1)} %param.6), channel_id=1, replica_groups=mesh['ctx'=8,'vocab_0'=4,'vocab_1'=4,'vocab_2'=2] {'ctx'}, dimensions={1}, use_global_device_ids=true | all-gather | bytes 589824 | tf_op jit(solution)/shard_map/all_gather | solution.py:49
  33.7 0.8 reshape.60
  34.5 0.8 reshape.61
  35.3 16.1 %all-gather.1 = s32[8,1,512]{2,1,0:T(1,128)S(1)} all-gather(s32[1,1,512]{2,1,0:T(1,128)S(1)} %bitcast.21), channel_id=2, replica_groups=mesh['ctx'=8,'vocab_0'=4,'vocab_1'=4,'vocab_2'=2] {'ctx'}, dimensions={0}, use_global_device_ids=true | all-gather | bytes 18432 | tf_op jit(solution)/shard_map/all_gather | solution.py:22
  51.8 0.8 compare_select_fusion.1
  52.6 71.6 %all-gather.4.cloned.1.call-done = bf16[2048,4096]{1,0:T(8,128)(2,1)} async-done(((bf16[2048,128]{1,0:T(8,128)(2,1)}), bf16[2048,4096]{1,0:T(8,128)(2,1)}) %all-gather.4.cloned.1.call-update) | async-done | bytes 16777232 | tf_op jit(solution)/shard_map/all_gather | solution.py:53
  124.2 14.8 %fusion.9 = (f32[2048]{0:T(1024)S(1)}, f32[2048,501]{0,1:T(8,128)}) fusion(bf16[2048,4096]{1,0:T(8,128)(2,1)} %all-gather.4.cloned.1.call-done, bf16[4096,501]{0,1:T(8,128)(2,1)} %param.7), kind=kOutput, calls=%fused_computation.35 | convolution fusion | flops 8406409216 | bytes 24993792 | tf_op jit(solution)/shard_map/dot_general | solution.py:54
  139.0 14.1 %pmax.28 = f32[2048]{0:T(1024)S(1)} all-reduce(f32[2048]{0:T(1024)S(1)} %get-tuple-element.29), channel_id=1, replica_groups=mesh['ctx'=8,'vocab_0'=4,'vocab_1'=4,'vocab_2'=2] {'ctx'}, use_global_device_ids=true, to_apply=%region_6.0 | all-reduce | flops 2048 | bytes 16384 | tf_op jit(solution)/shard_map/pmax | solution.py:32
  153.1 8.2 %pmax.29 = f32[2048]{0:T(1024)S(1)} all-reduce(f32[2048]{0:T(1024)S(1)} %pmax.28), channel_id=1, replica_groups=mesh['ctx'=8,'vocab_0'=4,'vocab_1'=4,'vocab_2'=2] {'vocab_0'}, use_global_device_ids=true, to_apply=%region_7.0 | all-reduce | flops 2048 | bytes 16384 | tf_op jit(solution)/shard_map/pmax | solution.py:32
  161.3 7.4 %pmax.30 = f32[2048]{0:T(1024)S(1)} all-reduce(f32[2048]{0:T(1024)S(1)} %pmax.29), channel_id=1, replica_groups=mesh['ctx'=8,'vocab_0'=4,'vocab_1'=4,'vocab_2'=2] {'vocab_1'}, use_global_device_ids=true, to_apply=%region_8.0 | all-reduce | flops 2048 | bytes 16384 | tf_op jit(solution)/shard_map/pmax | solution.py:32
  168.7 10.1 %pmax.31 = f32[2048]{0:T(1024)S(1)} all-reduce(f32[2048]{0:T(1024)S(1)} %pmax.30), channel_id=1, replica_groups=mesh['ctx'=8,'vocab_0'=4,'vocab_1'=4,'vocab_2'=2] {'vocab_2'}, use_global_device_ids=true, to_apply=%region_9.0 | all-reduce | flops 2048 | bytes 16384 | tf_op jit(solution)/shard_map/pmax | solution.py:32
  178.8 3.3 %exponential_reduce_fusion = (f32[2048]{0:T(1024)S(1)}, f32[2048]{0:T(1024)S(1)}) fusion(f32[2048,501]{0,1:T(8,128)} %get-tuple-element.30, f32[2048]{0:T(1024)S(1)} %pmax.31, s32[2048]{0:T(1024)S(1)} %sub.51), kind=kLoop, calls=%fused_computation.11 | loop fusion | flops 5126144 | bytes 4136960 | tf_op jit(solution)/shard_map/reduce_sum | solution.py:62
  182.1 20.5 %all-reduce = (f32[2048]{0:T(1024)S(1)}, f32[2048]{0:T(1024)S(1)}) all-reduce(f32[2048]{0:T(1024)S(1)} %get-tuple-element.5, f32[2048]{0:T(1024)S(1)} %get-tuple-element.4), channel_id=1, replica_groups=mesh['ctx'=8,'vocab_0'=4,'vocab_1'=4,'vocab_2'=2] {'ctx'}, use_global_device_ids=true, to_apply=%region_1.0 | all-reduce | flops 4096 | bytes 32768 | tf_op jit(solution)/shard_map/psum | solution.py:38
  202.6 10.8 %all-reduce.2 = (f32[2048]{0:T(1024)S(1)}, f32[2048]{0:T(1024)S(1)}) all-reduce(f32[2048]{0:T(1024)S(1)} %get-tuple-element.6, f32[2048]{0:T(1024)S(1)} %get-tuple-element.7), channel_id=1, replica_groups=mesh['ctx'=8,'vocab_0'=4,'vocab_1'=4,'vocab_2'=2] {'vocab_0'}, use_global_device_ids=true, to_apply=%region_2.0 | all-reduce | flops 4096 | bytes 32768 | tf_op jit(solution)/shard_map/psum | solution.py:38
  213.4 10.9 %all-reduce.1 = (f32[2048]{0:T(1024)S(1)}, f32[2048]{0:T(1024)S(1)}) all-reduce(f32[2048]{0:T(1024)S(1)} %get-tuple-element.10, f32[2048]{0:T(1024)S(1)} %get-tuple-element.11), channel_id=1, replica_groups=mesh['ctx'=8,'vocab_0'=4,'vocab_1'=4,'vocab_2'=2] {'vocab_1'}, use_global_device_ids=true, to_apply=%region_3.0 | all-reduce | flops 4096 | bytes 32768 | tf_op jit(solution)/shard_map/psum | solution.py:38
  224.3 17.9 %all-reduce.3 = (f32[2048]{0:T(1024)S(1)}, f32[2048]{0:T(1024)S(1)}) all-reduce(f32[2048]{0:T(1024)S(1)} %get-tuple-element.8, f32[2048]{0:T(1024)S(1)} %get-tuple-element.9), channel_id=1, replica_groups=mesh['ctx'=8,'vocab_0'=4,'vocab_1'=4,'vocab_2'=2] {'vocab_2'}, use_global_device_ids=true, to_apply=%region_4.0 | all-reduce | flops 4096 | bytes 32768 | tf_op jit(solution)/shard_map/psum | solution.py:38
  242.3 0.6 gather_fusion.1
  243.0 0.6 gather_fusion
  243.7 0.6 scatter_custom_fusion
  244.3 0.8 scatter_fusion
  245.1 3.5 %multiply_convert_fusion.1 = (bf16[2048,501]{0,1:T(8,128)(2,1)S(1)}, bf16[2048,501]{0,1:T(8,128)(2,1)S(1)}) fusion(f32[2048,501]{0,1:T(8,128)} %get-tuple-element.30, f32[2048]{0:T(1024)S(1)} %get-tuple-element.20, f32[2048]{0:T(1024)S(1)} %get-tuple-element.15, s32[2048]{0:T(1024)S(1)} %sub.51, f32[2048]{0:T(1024)S(1)} %get-tuple-element.14), kind=kLoop, calls=%fused_computation.9 | loop fusion | flops 8208384 | bytes 8241152 | tf_op jit(solution)/shard_map/convert_element_type | solution.py:78
  248.7 20.1 %convert_bitcast_fusion = bf16[4096,1002]{0,1:T(8,128)(2,1)S(1)} fusion(bf16[2048,4096]{1,0:T(8,128)(2,1)} %all-gather.4.cloned.1.call-done, bf16[2048,501]{0,1:T(8,128)(2,1)S(1)} %get-tuple-element.24, bf16[2048,501]{0,1:T(8,128)(2,1)S(1)} %get-tuple-element.23), kind=kOutput, calls=%fused_computation.4 | convolution fusion | flops 16823083008 | bytes 29089792 | tf_op jit(solution)/shard_map/dot_general | solution.py:43
  268.7 4.0 %fusion.8 = (bf16[4096,501]{0,1:T(8,128)(2,1)}, bf16[4096,501]{0,1:T(8,128)(2,1)}) fusion(bf16[4096,1002]{0,1:T(8,128)(2,1)S(1)} %convert_bitcast_fusion), kind=kLoop, calls=%fused_computation.34 | loop fusion | bytes 16416768 | tf_op jit(solution)/shard_map/slice | solution.py:83
  272.7 0.6 fusion.3
  (20 shorter events, 0.7 us)
Async XLA Ops:
  7.2 117.1 %all-gather.4.cloned.1.call-start = ((), (), s32[]{:S(2)}) async-start(), calls=%async_computation | async-start | bytes 17301504 | tf_op jit(solution)/shard_map/all_gather | solution.py:53
  139.0 103.3 %copy-start.1 = (f32[16]{0:T(128)S(1)}, f32[16]{0:T(128)}, u32[]{:S(2)}) copy-start(f32[16]{0:T(128)} %param.11) | copy-start | bytes 196
  243.6 29.1 %copy-start = (f32[8]{0:T(128)}, f32[8]{0:T(128)S(1)}, u32[]{:S(2)}) copy-start(f32[8]{0:T(128)S(1)} %get-tuple-element.18) | copy-start | bytes 100
Sparse Core Ops, SparseCore 0:
  33.8 90.3 all-gather.3
where the time goes:
time: 282 us
  blocking collectives  142 us (50%)
  waiting for transfers between devices  71.7 us (25%)
  matrix products  34.9 us (12%)
  between operations  15.9 us (6%)
  local copies, waits for them, and re-layouts  8.61 us (3%)
  other arithmetic  8.44 us (3%)
    all_gather x1, waiting for transfers between devices, shards(): whole_rows = lax.all_gather(token_rows, VOCAB, axis=1, tiled=True)  71.6 us
    psum x4, blocking collectives, by_axis_2(): shard = lax.psum(shard, axis)  60.1 us
    pmax x4, blocking collectives, by_axis(): shard = lax.pmax(shard, axis)  39.7 us
    all_gather x1, blocking collectives, shards(): seq_rows = lax.all_gather(hidden, 'ctx', axis=1, tiled=True)  26.5 us
    dot_general x1, matrix products, contract_rows(): lax.dot_general(block_rows, both_logits, (((0,), (0,)), ((), ())), prefer...  20.1 us
    all_gather x1, blocking collectives, gather_packed(): lines, at, finished = (lax.all_gather(flat, axis), 0, [])  16.1 us
    dot_general x1, matrix products, shards(): jnp.dot(whole_rows, head_weight, preferred_element_type=jnp.float32)  14.8 us
  transfers between devices with their start and end apart: 1, of which 1 were waited for; matrix products, arithmetic and copies ran while one was open for 1% of the time, Pallas kernels for 0%

commit v1 on v0

--- a/solution.py
+++ b/solution.py
@@ -50,7 +50,9 @@
     ids_all, mask_all = gather_packed((token_ids, response_mask), "ctx", (1, 1))
     token_rows = seq_rows.reshape(seq_rows.shape[0] * seq_rows.shape[1], seq_rows.shape[2])
     shard_width = head_weight.shape[1]
-    whole_rows = lax.all_gather(token_rows, VOCAB, axis=1, tiled=True)
+    whole_rows = jnp.concatenate(
+        lax.all_to_all(jnp.stack([token_rows] * lax.axis_size(VOCAB)), VOCAB, 0, 0), axis=1
+    )
     logits = jnp.dot(whole_rows, head_weight, preferred_element_type=jnp.float32)
     offset = lax.axis_index(CTX_VOCAB) * shard_width
     local_ids = ids_all.reshape(-1) - offset

time: 282 us -> 407 us (1.44)
  waiting for transfers between devices: 71.7 us -> 183 us
  starting transfers between devices: 0.04 us -> 14.1 us
  between operations: 15.9 us -> 2.58 us
  blocking collectives: 142 us -> 151 us
  local copies, waits for them, and re-layouts: 8.61 us -> 13.4 us
    all_to_all x0 -> x1, waiting for transfers between devices: none -> 183 us  [shards(): lax.all_to_all(jnp.stack([token_rows] * lax.axis_size(VOCAB)), VOCAB, 0, 0)]
    all_gather x1 -> x0, waiting for transfers between devices: 71.6 us -> none  [shards(): whole_rows = lax.all_gather(token_rows, VOCAB, axis=1, tiled=True)]
    all_to_all x0 -> x1, starting transfers between devices: none -> 14.1 us  [shards(): lax.all_to_all(jnp.stack([token_rows] * lax.axis_size(VOCAB)), VOCAB, 0, 0)]
    another operation x0 -> x2, local copies, waits for them, and re-layouts: none -> 6.2 us  [shards(): jnp.stack([token_rows] * lax.axis_size(VOCAB))]
    pmax x4, blocking collectives: 39.7 us -> 45.8 us  [by_axis(): shard = lax.pmax(shard, axis)]
  transfers between devices with their start and end apart: 1 -> 1, of which waited for: 1 -> 1; matrix products, arithmetic and copies ran while one was open for 1% -> 0% of each run, Pallas kernels for 0% -> 0%
where the time goes in v1:
time: 407 us
  waiting for transfers between devices  183 us (45%)
  blocking collectives  151 us (37%)
  matrix products  34.8 us (9%)
  starting transfers between devices  14.1 us (3%)
  local copies, waits for them, and re-layouts  13.4 us (3%)
  other arithmetic  7.71 us (2%)
    all_to_all x1, waiting for transfers between devices, shards(): lax.all_to_all(jnp.stack([token_rows] * lax.axis_size(VOCAB)), VOCAB, 0, 0)  183 us
    psum x4, blocking collectives, by_axis_2(): shard = lax.psum(shard, axis)  62.8 us
    pmax x4, blocking collectives, by_axis(): shard = lax.pmax(shard, axis)  45.8 us
    all_gather x1, blocking collectives, shards(): seq_rows = lax.all_gather(hidden, 'ctx', axis=1, tiled=True)  23.9 us
    dot_general x1, matrix products, contract_rows(): lax.dot_general(block_rows, both_logits, (((0,), (0,)), ((), ())), prefer...  20.1 us
    all_gather x1, blocking collectives, gather_packed(): lines, at, finished = (lax.all_gather(flat, axis), 0, [])  18.6 us
    dot_general x1, matrix products, shards(): jnp.dot(whole_rows, head_weight, preferred_element_type=jnp.float32)  14.7 us
    all_to_all x1, starting transfers between devices, shards(): lax.all_to_all(jnp.stack([token_rows] * lax.axis_size(VOCAB)), VOCAB, 0, 0)  14.1 us
  transfers between devices with their start and end apart: 1, of which 1 were waited for; matrix products, arithmetic and copies ran while one was open for 0% of the time, Pallas kernels for 0%

profile of v1, /device:TPU:1, one launch (start us, length us, event | category | flops | bytes accessed | tf_op | source)
XLA Modules:
  0.0 406.6 jit_solution(15621872713579685416)
XLA Ops:
  0.6 23.9 %all_gather.11 = bf16[16,128,128]{2,1,0:T(8,128)(2,1)S(1)} all-gather(bf16[16,16,128]{2,1,0:T(8,128)(2,1)} %param.6), channel_id=1, replica_groups=mesh['ctx'=8,'vocab_0'=4,'vocab_1'=4,'vocab_2'=2] {'ctx'}, dimensions={1}, use_global_device_ids=true | all-gather | bytes 589824 | tf_op jit(solution)/shard_map/all_gather | solution.py:49
  24.6 0.2 copy.18
  24.8 6.0 %stack.3 = bf16[32,2048,128]{1,2,0:T(8,128)(2,1)} broadcast(bf16[2048,128]{0,1:T(8,128)(2,1)S(1)} %copy.18), dimensions={1,2} | broadcast | bytes 17301504 | tf_op jit(solution)/shard_map/stack | solution.py:54
  30.8 14.1 %all-to-all-start = ((bf16[32,2048,128]{1,2,0:T(8,128)(2,1)}), bf16[32,2048,128]{1,2,0:T(8,128)(2,1)}, u32[]{:S(2)}, u32[]{:S(2)}) async-start(bf16[32,2048,128]{1,2,0:T(8,128)(2,1)} %stack.3), calls=%async_computation | async-start | bytes 33554432 | tf_op jit(solution)/shard_map/all_to_all | solution.py:54
  45.1 18.6 %all-gather.1 = s32[8,1,512]{2,1,0:T(1,128)S(1)} all-gather(s32[1,1,512]{2,1,0:T(1,128)S(1)} %bitcast.24), channel_id=2, replica_groups=mesh['ctx'=8,'vocab_0'=4,'vocab_1'=4,'vocab_2'=2] {'ctx'}, dimensions={0}, use_global_device_ids=true | all-gather | bytes 18432 | tf_op jit(solution)/shard_map/all_gather | solution.py:22
  64.2 182.8 %all-to-all-done = bf16[32,2048,128]{1,2,0:T(8,128)(2,1)} async-done(((bf16[32,2048,128]{1,2,0:T(8,128)(2,1)}), bf16[32,2048,128]{1,2,0:T(8,128)(2,1)}, u32[]{:S(2)}, u32[]{:S(2)}) %all-to-all-start) | async-done | bytes 16777248 | tf_op jit(solution)/shard_map/all_to_all | solution.py:54
  247.0 14.7 %fusion.9 = (f32[2048]{0:T(1024)S(1)}, f32[2048,501]{0,1:T(8,128)}) fusion(bf16[2048,4096]{0,1:T(8,128)(2,1)} %bitcast.4, bf16[4096,501]{0,1:T(8,128)(2,1)} %param.7), kind=kOutput, calls=%fused_computation.35 | convolution fusion | flops 8406409216 | bytes 24993792 | tf_op jit(solution)/shard_map/dot_general | solution.py:56
  261.7 12.7 %pmax.28 = f32[2048]{0:T(1024)S(1)} all-reduce(f32[2048]{0:T(1024)S(1)} %get-tuple-element.29), channel_id=1, replica_groups=mesh['ctx'=8,'vocab_0'=4,'vocab_1'=4,'vocab_2'=2] {'ctx'}, use_global_device_ids=true, to_apply=%region_6.0 | all-reduce | flops 2048 | bytes 16384 | tf_op jit(solution)/shard_map/pmax | solution.py:32
  274.5 6.1 %pmax.29 = f32[2048]{0:T(1024)S(1)} all-reduce(f32[2048]{0:T(1024)S(1)} %pmax.28), channel_id=1, replica_groups=mesh['ctx'=8,'vocab_0'=4,'vocab_1'=4,'vocab_2'=2] {'vocab_0'}, use_global_device_ids=true, to_apply=%region_7.0 | all-reduce | flops 2048 | bytes 16384 | tf_op jit(solution)/shard_map/pmax | solution.py:32
  280.6 18.0 %pmax.30 = f32[2048]{0:T(1024)S(1)} all-reduce(f32[2048]{0:T(1024)S(1)} %pmax.29), channel_id=1, replica_groups=mesh['ctx'=8,'vocab_0'=4,'vocab_1'=4,'vocab_2'=2] {'vocab_1'}, use_global_device_ids=true, to_apply=%region_8.0 | all-reduce | flops 2048 | bytes 16384 | tf_op jit(solution)/shard_map/pmax | solution.py:32
  298.6 9.0 %pmax.31 = f32[2048]{0:T(1024)S(1)} all-reduce(f32[2048]{0:T(1024)S(1)} %pmax.30), channel_id=1, replica_groups=mesh['ctx'=8,'vocab_0'=4,'vocab_1'=4,'vocab_2'=2] {'vocab_2'}, use_global_device_ids=true, to_apply=%region_9.0 | all-reduce | flops 2048 | bytes 16384 | tf_op jit(solution)/shard_map/pmax | solution.py:32
  307.6 3.3 exponential_reduce_fusion
  310.8 20.1 %all-reduce = (f32[2048]{0:T(1024)S(1)}, f32[2048]{0:T(1024)S(1)}) all-reduce(f32[2048]{0:T(1024)S(1)} %get-tuple-element.5, f32[2048]{0:T(1024)S(1)} %get-tuple-element.4), channel_id=1, replica_groups=mesh['ctx'=8,'vocab_0'=4,'vocab_1'=4,'vocab_2'=2] {'ctx'}, use_global_device_ids=true, to_apply=%region_1.0 | all-reduce | flops 4096 | bytes 32768 | tf_op jit(solution)/shard_map/psum | solution.py:38
  330.9 12.4 %all-reduce.2 = (f32[2048]{0:T(1024)S(1)}, f32[2048]{0:T(1024)S(1)}) all-reduce(f32[2048]{0:T(1024)S(1)} %get-tuple-element.6, f32[2048]{0:T(1024)S(1)} %get-tuple-element.7), channel_id=1, replica_groups=mesh['ctx'=8,'vocab_0'=4,'vocab_1'=4,'vocab_2'=2] {'vocab_0'}, use_global_device_ids=true, to_apply=%region_2.0 | all-reduce | flops 4096 | bytes 32768 | tf_op jit(solution)/shard_map/psum | solution.py:38
  343.3 12.4 %all-reduce.1 = (f32[2048]{0:T(1024)S(1)}, f32[2048]{0:T(1024)S(1)}) all-reduce(f32[2048]{0:T(1024)S(1)} %get-tuple-element.10, f32[2048]{0:T(1024)S(1)} %get-tuple-element.11), channel_id=1, replica_groups=mesh['ctx'=8,'vocab_0'=4,'vocab_1'=4,'vocab_2'=2] {'vocab_1'}, use_global_device_ids=true, to_apply=%region_3.0 | all-reduce | flops 4096 | bytes 32768 | tf_op jit(solution)/shard_map/psum | solution.py:38
  355.7 17.9 %all-reduce.3 = (f32[2048]{0:T(1024)S(1)}, f32[2048]{0:T(1024)S(1)}) all-reduce(f32[2048]{0:T(1024)S(1)} %get-tuple-element.8, f32[2048]{0:T(1024)S(1)} %get-tuple-element.9), channel_id=1, replica_groups=mesh['ctx'=8,'vocab_0'=4,'vocab_1'=4,'vocab_2'=2] {'vocab_2'}, use_global_device_ids=true, to_apply=%region_4.0 | all-reduce | flops 4096 | bytes 32768 | tf_op jit(solution)/shard_map/psum | solution.py:38
  373.8 0.6 gather_fusion.1
  374.4 0.6 gather_fusion
  375.1 0.6 scatter_custom_fusion
  375.7 0.8 scatter_fusion
  376.6 3.5 multiply_convert_fusion.1
  380.1 20.1 %convert_bitcast_fusion = bf16[4096,1002]{0,1:T(8,128)(2,1)S(1)} fusion(bf16[2048,4096]{0,1:T(8,128)(2,1)} %bitcast.4, bf16[2048,501]{0,1:T(8,128)(2,1)S(1)} %get-tuple-element.24, bf16[2048,501]{0,1:T(8,128)(2,1)S(1)} %get-tuple-element.23), kind=kOutput, calls=%fused_computation.4 | convolution fusion | flops 16823083008 | bytes 29089792 | tf_op jit(solution)/shard_map/dot_general | solution.py:43
  400.2 4.0 fusion.8
  404.3 0.6 fusion.3
  (27 shorter events, 0.9 us)
Async XLA Ops:
  30.8 14.2 %copy-start = (s32[16,16]{1,0:T(8,128)S(1)}, s32[16,16]{1,0:T(8,128)}, u32[]{:S(2)}) copy-start(s32[16,16]{1,0:T(8,128)} %param.8) | copy-start | bytes 3076
  30.8 14.3 %copy-start.1 = (s32[16,16]{1,0:T(8,128)S(1)}, s32[16,16]{1,0:T(8,128)}, u32[]{:S(2)}) copy-start(s32[16,16]{1,0:T(8,128)} %param.9) | copy-start | bytes 3076
  30.8 33.4 %copy-start.2 = (s32[16]{0:T(128)S(1)}, s32[16]{0:T(128)}, u32[]{:S(2)}) copy-start(s32[16]{0:T(128)} %param.10) | copy-start | bytes 196
  30.8 216.2 %all-to-all-start = ((bf16[32,2048,128]{1,2,0:T(8,128)(2,1)}), bf16[32,2048,128]{1,2,0:T(8,128)(2,1)}, u32[]{:S(2)}, u32[]{:S(2)}) async-start(bf16[32,2048,128]{1,2,0:T(8,128)(2,1)} %stack.3), calls=%async_computation | async-start | bytes 33554432 | tf_op jit(solution)/shard_map/all_to_all | solution.py:54
  261.7 112.0 %copy-start.4 = (f32[16]{0:T(128)S(1)}, f32[16]{0:T(128)}, u32[]{:S(2)}) copy-start(f32[16]{0:T(128)} %param.11) | copy-start | bytes 196
  375.1 29.2 %copy-start.3 = (f32[8]{0:T(128)}, f32[8]{0:T(128)S(1)}, u32[]{:S(2)}) copy-start(f32[8]{0:T(128)S(1)} %get-tuple-element.18) | copy-start | bytes 100
